TPU v7x, 8 devices: a whole 2x2x1 slice. The times are simulated.
8 devices in a mesh: third: 2 (over z, y), second: 2 (over x), group: 2 (over core).
Axes of the slice: x: 2, y: 2, z: 1, core: 2. Of those that a mesh axis runs over, the one named last changes fastest.
Arguments:
- x_one: bfloat16 [32768, 1024], P(('third', 'second', 'group'))
- z_one: bfloat16 [32768, 4096], P(('third', 'second', 'group'))
- x_two: bfloat16 [32768, 1024], P(('third', 'second', 'group'))
- z_two: bfloat16 [32768, 4096], P(('third', 'second', 'group'))
- grad_out: bfloat16 [32768, 1024], P(('third', 'second', 'group'))
- w1_in: bfloat16 [1024, 4096], replicated
- w1_out: bfloat16 [4096, 1024], replicated
- w2_in: bfloat16 [1024, 4096], replicated
- w2_out: bfloat16 [4096, 1024], replicated
Outputs:
- output 1: float32 [4096, 1024], replicated
- output 2: float32 [1024, 4096], replicated
- output 3: float32 [4096, 1024], replicated
- output 4: float32 [1024, 4096], replicated
- output 5: bfloat16 [32768, 1024], P(('third', 'second', 'group'))
All inputs are finite; a program needn't handle non-finite values.
Results may differ from a plain program's by a relative error of at most 0.00511536.
Values are sent between devices in bfloat16 or wider.
A program may use at most 1 GiB of HBM per device.

v0:
```python
import math
import jax
import jax.numpy as jnp
from jax import lax
from jax.sharding import PartitionSpec as P

AXES = ('third', 'second', 'group')
INV_ROOT_TWO = math.sqrt(0.5)
INV_ROOT_TWO_PI = 1.0 / math.sqrt(2.0 * math.pi)
CONTRACT_ROWS = (((0,), (0,)), ((), ()))
CONTRACT_COLS = (((1,), (1,)), ((), ()))


def gelu_pair(z_pre):
    z_val = z_pre.astype(jnp.float32)
    cdf_val = 0.5 * (1.0 + lax.erf(z_val * INV_ROOT_TWO))
    hidden = (z_val * cdf_val).astype(jnp.bfloat16)
    slope = cdf_val + z_val * jnp.exp(-0.5 * z_val * z_val) * INV_ROOT_TWO_PI
    return hidden, slope


def block_backward(x_in, z_pre, grad_y, w_in, w_out):
    hidden, slope = gelu_pair(z_pre)
    w_out_grad = lax.dot_general(hidden, grad_y, CONTRACT_ROWS, preferred_element_type=jnp.float32).astype(jnp.bfloat16)
    grad_hidden = lax.dot_general(grad_y, w_out, CONTRACT_COLS, preferred_element_type=jnp.float32)
    grad_pre = (grad_hidden * slope).astype(jnp.bfloat16)
    w_in_grad = lax.dot_general(x_in, grad_pre, CONTRACT_ROWS, preferred_element_type=jnp.float32).astype(jnp.bfloat16)
    grad_x = (grad_y.astype(jnp.float32) + lax.dot_general(grad_pre, w_in, CONTRACT_COLS, preferred_element_type=jnp.float32)).astype(jnp.bfloat16)
    return w_out_grad, w_in_grad, grad_x


def reduce_grad(grad, group_size):
    row_count, col_count = grad.shape
    pieces = grad.reshape(group_size, row_count // group_size, col_count)
    received = lax.all_to_all(pieces, 'group', 0, 0)
    part_sum = jnp.sum(received, axis=0, dtype=jnp.float32)
    part_sum = lax.psum_scatter(part_sum, 'second', scatter_dimension=0, tiled=True)
    part_sum = lax.psum_scatter(part_sum, 'third', scatter_dimension=0, tiled=True)
    full_sum = lax.all_gather(part_sum, 'third', axis=0, tiled=True)
    full_sum = lax.all_gather(full_sum, 'second', axis=0, tiled=True)
    return lax.all_gather(full_sum, 'group', axis=0, tiled=True)


def solution(mesh):
    group_size = mesh.shape['group']

    def device_step(x_one, z_one, x_two, z_two, grad_out, w1_in, w1_out, w2_in, w2_out):
        w2o_grad, w2i_grad, dx_two = block_backward(x_two, z_two, grad_out, w2_in, w2_out)
        sum_w2o = reduce_grad(w2o_grad, group_size)
        sum_w2i = reduce_grad(w2i_grad, group_size)
        w1o_grad, w1i_grad, dx_one = block_backward(x_one, z_one, dx_two, w1_in, w1_out)
        sum_w1o = reduce_grad(w1o_grad, group_size)
        sum_w1i = reduce_grad(w1i_grad, group_size)
        return sum_w2o, sum_w2i, sum_w1o, sum_w1i, dx_one

    row_spec = P(AXES, None)
    repl_spec = P()
    return jax.shard_map(
        device_step,
        mesh=mesh,
        in_specs=(row_spec, row_spec, row_spec, row_spec, row_spec, repl_spec, repl_spec, repl_spec, repl_spec),
        out_specs=(repl_spec, repl_spec, repl_spec, repl_spec, row_spec),
        check_vma=False,
    )
```

profile of v0, /device:TPU:0, one launch (start us, length us, event | category | flops | bytes accessed | tf_op | source)
XLA Modules:
  0.0 1673.0 jit_solution(13347076267672013108)
XLA Ops:
  7.2 0.0 reduce-scatter.21.cloned.1.call-start
  7.2 64.9 %fusion.8 = bf16[4096,4096]{1,0:T(8,128)(2,1)} fusion(bf16[4096,4096]{1,0:T(8,128)(2,1)} %param.12, bf16[4096,1024]{1,0:T(8,128)(2,1)} %param.13, bf16[4096,1024]{1,0:T(8,128)(2,1)} %param.17), kind=kOutput, calls=%fused_computation.18 | convolution fusion | flops 34544287744 | bytes 83886080 | tf_op jit(solution)/shard_map/dot_general | solution.py:25
  72.1 43.1 %add_convert_fusion.1 = bf16[4096,1024]{1,0:T(8,128)(2,1)} fusion(bf16[4096,1024]{1,0:T(8,128)(2,1)} %param.13, bf16[4096,4096]{1,0:T(8,128)(2,1)} %fusion.8, bf16[1024,4096]{1,0:T(8,128)(2,1)} %param.16), kind=kOutput, calls=%fused_computation.33 | convolution fusion | flops 34372321280 | bytes 58720256 | tf_op jit(solution)/shard_map/dot_general | solution.py:28
  115.2 65.4 %fusion.17 = bf16[4096,4096]{1,0:T(8,128)(2,1)} fusion(bf16[4096,4096]{1,0:T(8,128)(2,1)} %param.10, bf16[4096,1024]{1,0:T(8,128)(2,1)} %add_convert_fusion.1, bf16[4096,1024]{1,0:T(8,128)(2,1)} %param.15), kind=kOutput, calls=%fused_computation.27 | convolution fusion | flops 34544287744 | bytes 83886080 | tf_op jit(solution)/shard_map/dot_general | solution.py:25
  180.6 43.1 %convolution_convert_fusion = bf16[4096,1024]{0,1:T(8,128)(2,1)} fusion(bf16[4096,4096]{1,0:T(8,128)(2,1)} %fusion.17, bf16[4096,1024]{1,0:T(8,128)(2,1)} %param.9), kind=kOutput, calls=%fused_computation.38 | convolution fusion | flops 34363932672 | bytes 50331648 | tf_op jit(solution)/shard_map/dot_general | solution.py:27
  223.7 18.6 %all_to_all.20 = bf16[2,512,4096]{2,1,0:T(8,128)(2,1)} all-to-all(bf16[2,512,4096]{2,1,0:T(8,128)(2,1)} %bitcast.28), channel_id=1, replica_groups=mesh['third'=2,'second'=2,'group'=2] {'group'}, dimensions={0} | all-to-all | bytes 16777216 | tf_op jit(solution)/shard_map/all_to_all | solution.py:35
  242.3 9.6 convert_reduce_fusion
  251.9 0.0 reduce-scatter.21.cloned.1.call-update
  251.9 0.0 reduce-scatter.17.cloned.1.call-start
  251.9 45.6 %fusion.25 = bf16[4096,1024]{1,0:T(8,128)(2,1)S(1)} fusion(bf16[4096,1024]{1,0:T(8,128)(2,1)} %add_convert_fusion.1, bf16[4096,4096]{1,0:T(8,128)(2,1)} %param.10), kind=kOutput, calls=%fused_computation.37 | convolution fusion | flops 34464595968 | bytes 50331648 | tf_op jit(solution)/shard_map/dot_general | solution.py:24
  297.6 11.7 all_to_all.21
  309.3 10.0 convert_reduce_fusion.1
  319.3 0.0 reduce-scatter.13.cloned.1.call-start
  319.4 43.1 %convolution_convert_fusion.1 = bf16[4096,1024]{0,1:T(8,128)(2,1)} fusion(bf16[4096,4096]{1,0:T(8,128)(2,1)} %fusion.8, bf16[4096,1024]{1,0:T(8,128)(2,1)} %param.11), kind=kOutput, calls=%fused_computation.39 | convolution fusion | flops 34363932672 | bytes 50331648 | tf_op jit(solution)/shard_map/dot_general | solution.py:27
  362.5 18.2 %all_to_all.22 = bf16[2,512,4096]{2,1,0:T(8,128)(2,1)} all-to-all(bf16[2,512,4096]{2,1,0:T(8,128)(2,1)} %bitcast.27), channel_id=1, replica_groups=mesh['third'=2,'second'=2,'group'=2] {'group'}, dimensions={0} | all-to-all | bytes 16777216 | tf_op jit(solution)/shard_map/all_to_all | solution.py:35
  380.6 9.6 convert_reduce_fusion.2
  390.3 0.0 reduce-scatter.9.cloned.1.call-start
  390.3 45.4 %fusion.22 = bf16[4096,1024]{1,0:T(8,128)(2,1)S(1)} fusion(bf16[4096,1024]{1,0:T(8,128)(2,1)} %param.13, bf16[4096,4096]{1,0:T(8,128)(2,1)} %param.12), kind=kOutput, calls=%fused_computation.36 | convolution fusion | flops 34464595968 | bytes 50331648 | tf_op jit(solution)/shard_map/dot_general | solution.py:24
  435.7 12.0 all_to_all.23
  447.7 10.0 convert_reduce_fusion.3
  457.8 0.0 reduce-scatter.23.cloned.1.call-start
  457.8 0.0 reduce-scatter.21.cloned.1.call-done
  457.9 0.5 reduce-scatter.23.cloned.1.call-update
  458.4 0.0 reduce-scatter.19.cloned.1.call-start
  458.4 0.0 reduce-scatter.17.cloned.1.call-done
  458.4 0.5 reduce-scatter.19.cloned.1.call-update
  458.9 0.0 reduce-scatter.15.cloned.1.call-start
  459.0 90.6 %reduce-scatter.13.cloned.1.call-done = f32[256,4096]{1,0:T(8,128)} async-done(((f32[512,4096]{1,0:T(8,128)}), f32[256,4096]{1,0:T(8,128)}) %reduce-scatter.13.cloned.1.call-update) | async-done | bytes 4194320 | tf_op jit(solution)/shard_map/reduce_scatter | solution.py:37
  549.6 0.0 reduce-scatter.11.cloned.1.call-start
  549.7 99.1 %reduce-scatter.9.cloned.1.call-done = f32[1024,1024]{1,0:T(8,128)} async-done(((f32[2048,1024]{1,0:T(8,128)}), f32[1024,1024]{1,0:T(8,128)}) %reduce-scatter.9.cloned.1.call-update) | async-done | bytes 4194320 | tf_op jit(solution)/shard_map/reduce_scatter | solution.py:37
  648.8 0.0 all-gather.31.cloned.1.call-start
  648.8 53.6 %reduce-scatter.23.cloned.1.call-done = f32[128,4096]{1,0:T(8,128)} async-done(((f32[256,4096]{1,0:T(8,128)}), f32[128,4096]{1,0:T(8,128)}) %reduce-scatter.23.cloned.1.call-update) | async-done | bytes 2097168 | tf_op jit(solution)/shard_map/reduce_scatter | solution.py:38
  702.4 0.0 all-gather.25.cloned.1.call-start
  702.5 53.6 %reduce-scatter.19.cloned.1.call-done = f32[512,1024]{1,0:T(8,128)} async-done(((f32[1024,1024]{1,0:T(8,128)}), f32[512,1024]{1,0:T(8,128)}) %reduce-scatter.19.cloned.1.call-update) | async-done | bytes 2097168 | tf_op jit(solution)/shard_map/reduce_scatter | solution.py:38
  756.1 0.0 all-gather.19.cloned.1.call-start
  756.1 53.7 %reduce-scatter.15.cloned.1.call-done = f32[128,4096]{1,0:T(8,128)} async-done(((f32[256,4096]{1,0:T(8,128)}), f32[128,4096]{1,0:T(8,128)}) %reduce-scatter.15.cloned.1.call-update) | async-done | bytes 2097168 | tf_op jit(solution)/shard_map/reduce_scatter | solution.py:38
  809.9 0.0 all-gather.13.cloned.1.call-start
  809.9 53.7 %reduce-scatter.11.cloned.1.call-done = f32[512,1024]{1,0:T(8,128)} async-done(((f32[1024,1024]{1,0:T(8,128)}), f32[512,1024]{1,0:T(8,128)}) %reduce-scatter.11.cloned.1.call-update) | async-done | bytes 2097168 | tf_op jit(solution)/shard_map/reduce_scatter | solution.py:38
  863.6 0.0 all-gather.33.cloned.1.call-start
  863.7 55.7 %all-gather.31.cloned.1.call-done = f32[256,4096]{1,0:T(8,128)} async-done(((f32[128,4096]{1,0:T(8,128)}), f32[256,4096]{1,0:T(8,128)}) %all-gather.31.cloned.1.call-update) | async-done | bytes 4194320 | tf_op jit(solution)/shard_map/all_gather | solution.py:39
  919.4 0.0 all-gather.27.cloned.1.call-start
  919.4 55.5 %all-gather.25.cloned.1.call-done = f32[1024,1024]{1,0:T(8,128)} async-done(((f32[512,1024]{1,0:T(8,128)}), f32[1024,1024]{1,0:T(8,128)}) %all-gather.25.cloned.1.call-update) | async-done | bytes 4194320 | tf_op jit(solution)/shard_map/all_gather | solution.py:39
  974.9 0.0 all-gather.21.cloned.1.call-start
  975.0 55.7 %all-gather.19.cloned.1.call-done = f32[256,4096]{1,0:T(8,128)} async-done(((f32[128,4096]{1,0:T(8,128)}), f32[256,4096]{1,0:T(8,128)}) %all-gather.19.cloned.1.call-update) | async-done | bytes 4194320 | tf_op jit(solution)/shard_map/all_gather | solution.py:39
  1030.7 0.0 all-gather.15.cloned.1.call-start
  1030.7 55.5 %all-gather.13.cloned.1.call-done = f32[1024,1024]{1,0:T(8,128)} async-done(((f32[512,1024]{1,0:T(8,128)}), f32[1024,1024]{1,0:T(8,128)}) %all-gather.13.cloned.1.call-update) | async-done | bytes 4194320 | tf_op jit(solution)/shard_map/all_gather | solution.py:39
  1086.2 0.0 all-gather.35.cloned.1.call-start
  1086.3 103.7 %all-gather.33.cloned.1.call-done = f32[512,4096]{1,0:T(8,128)} async-done(((f32[256,4096]{1,0:T(8,128)}), f32[512,4096]{1,0:T(8,128)}) %all-gather.33.cloned.1.call-update) | async-done | bytes 8388624 | tf_op jit(solution)/shard_map/all_gather | solution.py:40
  1190.1 0.0 all-gather.29.cloned.1.call-start
  1190.1 103.6 %all-gather.27.cloned.1.call-done = f32[2048,1024]{1,0:T(8,128)} async-done(((f32[1024,1024]{1,0:T(8,128)}), f32[2048,1024]{1,0:T(8,128)}) %all-gather.27.cloned.1.call-update) | async-done | bytes 8388624 | tf_op jit(solution)/shard_map/all_gather | solution.py:40
  1293.7 0.0 all-gather.23.cloned.1.call-start
  1293.8 103.6 %all-gather.21.cloned.1.call-done = f32[512,4096]{1,0:T(8,128)} async-done(((f32[256,4096]{1,0:T(8,128)}), f32[512,4096]{1,0:T(8,128)}) %all-gather.21.cloned.1.call-update) | async-done | bytes 8388624 | tf_op jit(solution)/shard_map/all_gather | solution.py:40
  1397.4 0.0 all-gather.17.cloned.1.call-start
  1397.4 103.6 %all-gather.15.cloned.1.call-done = f32[2048,1024]{1,0:T(8,128)} async-done(((f32[1024,1024]{1,0:T(8,128)}), f32[2048,1024]{1,0:T(8,128)}) %all-gather.15.cloned.1.call-update) | async-done | bytes 8388624 | tf_op jit(solution)/shard_map/all_gather | solution.py:40
  1501.0 42.9 %add_convert_fusion = bf16[4096,1024]{1,0:T(8,128)(2,1)} fusion(bf16[4096,1024]{1,0:T(8,128)(2,1)} %add_convert_fusion.1, bf16[4096,4096]{1,0:T(8,128)(2,1)} %fusion.17, bf16[1024,4096]{1,0:T(8,128)(2,1)} %param.14), kind=kOutput, calls=%fused_computation.30 | convolution fusion | flops 34372321280 | bytes 58720256 | tf_op jit(solution)/shard_map/dot_general | solution.py:28
  1543.9 16.7 all-gather.29.cloned.1.call-done
  1560.6 30.5 %all-gather.23.cloned.1.call-done = f32[1024,4096]{1,0:T(8,128)} async-done(((f32[512,4096]{1,0:T(8,128)}), f32[1024,4096]{1,0:T(8,128)}) %all-gather.23.cloned.1.call-update) | async-done | bytes 16777232 | tf_op jit(solution)/shard_map/all_gather | solution.py:41
  1591.1 30.4 %all-gather.17.cloned.1.call-done = f32[4096,1024]{1,0:T(8,128)} async-done(((f32[2048,1024]{1,0:T(8,128)}), f32[4096,1024]{1,0:T(8,128)}) %all-gather.17.cloned.1.call-update) | async-done | bytes 16777232 | tf_op jit(solution)/shard_map/all_gather | solution.py:41
  1621.5 13.0 copy.18
  1634.5 13.5 copy.19
  1648.1 8.5 copy.20
  1656.6 1.8 slice-done.2
  1658.3 1.2 slice-done.3
  1659.5 6.2 copy.21
  (34 shorter events, 0.3 us)
Async XLA Ops:
  7.2 450.7 %reduce-scatter.21.cloned.1.call-start = ((), (), s32[]{:S(2)}) async-start(), calls=%async_computation.27 | async-start | bytes 12582912 | tf_op jit(solution)/shard_map/reduce_scatter | solution.py:37
  251.9 206.5 %reduce-scatter.17.cloned.1.call-start = ((), (), s32[]{:S(2)}) async-start(), calls=%async_computation.22 | async-start | bytes 12582912 | tf_op jit(solution)/shard_map/reduce_scatter | solution.py:37
  319.3 230.3 %reduce-scatter.13.cloned.1.call-start = ((), (), s32[]{:S(2)}) async-start(), calls=%async_computation.17 | async-start | bytes 12582912 | tf_op jit(solution)/shard_map/reduce_scatter | solution.py:37
  390.3 258.5 %reduce-scatter.9.cloned.1.call-start = ((), (), s32[]{:S(2)}) async-start(), calls=%async_computation.12 | async-start | bytes 12582912 | tf_op jit(solution)/shard_map/reduce_scatter | solution.py:37
  457.8 244.6 %reduce-scatter.23.cloned.1.call-start = ((), (), s32[]{:S(2)}) async-start(), calls=%async_computation.28 | async-start | bytes 6291456 | tf_op jit(solution)/shard_map/reduce_scatter | solution.py:38
  458.4 297.7 %reduce-scatter.19.cloned.1.call-start = ((), (), s32[]{:S(2)}) async-start(), calls=%async_computation.23 | async-start | bytes 6291456 | tf_op jit(solution)/shard_map/reduce_scatter | solution.py:38
  458.9 350.9 %reduce-scatter.15.cloned.1.call-start = ((), (), s32[]{:S(2)}) async-start(), calls=%async_computation.18 | async-start | bytes 6291456 | tf_op jit(solution)/shard_map/reduce_scatter | solution.py:38
  549.6 314.0 %reduce-scatter.11.cloned.1.call-start = ((), (), s32[]{:S(2)}) async-start(), calls=%async_computation.13 | async-start | bytes 6291456 | tf_op jit(solution)/shard_map/reduce_scatter | solution.py:38
  648.8 270.6 %all-gather.31.cloned.1.call-start = ((), (), s32[]{:S(2)}) async-start(), calls=%async_computation.29 | async-start | bytes 6291456 | tf_op jit(solution)/shard_map/all_gather | solution.py:39
  702.4 272.5 %all-gather.25.cloned.1.call-start = ((), (), s32[]{:S(2)}) async-start(), calls=%async_computation.24 | async-start | bytes 6291456 | tf_op jit(solution)/shard_map/all_gather | solution.py:39
  756.1 274.6 %all-gather.19.cloned.1.call-start = ((), (), s32[]{:S(2)}) async-start(), calls=%async_computation.19 | async-start | bytes 6291456 | tf_op jit(solution)/shard_map/all_gather | solution.py:39
  809.9 276.4 %all-gather.13.cloned.1.call-start = ((), (), s32[]{:S(2)}) async-start(), calls=%async_computation.14 | async-start | bytes 6291456 | tf_op jit(solution)/shard_map/all_gather | solution.py:39
  863.6 326.4 %all-gather.33.cloned.1.call-start = ((), (), s32[]{:S(2)}) async-start(), calls=%async_computation.30 | async-start | bytes 12582912 | tf_op jit(solution)/shard_map/all_gather | solution.py:40
  919.4 374.3 %all-gather.27.cloned.1.call-start = ((), (), s32[]{:S(2)}) async-start(), calls=%async_computation.25 | async-start | bytes 12582912 | tf_op jit(solution)/shard_map/all_gather | solution.py:40
  974.9 422.4 %all-gather.21.cloned.1.call-start = ((), (), s32[]{:S(2)}) async-start(), calls=%async_computation.20 | async-start | bytes 12582912 | tf_op jit(solution)/shard_map/all_gather | solution.py:40
  1030.7 470.3 %all-gather.15.cloned.1.call-start = ((), (), s32[]{:S(2)}) async-start(), calls=%async_computation.15 | async-start | bytes 12582912 | tf_op jit(solution)/shard_map/all_gather | solution.py:40
  1086.2 457.7 %all-gather.35.cloned.1.call-start = ((), (), s32[]{:S(2)}) async-start(), calls=%async_computation.31 | async-start | bytes 25165824 | tf_op jit(solution)/shard_map/all_gather | solution.py:41
  1190.1 370.6 %all-gather.29.cloned.1.call-start = ((), (), s32[]{:S(2)}) async-start(), calls=%async_computation.26 | async-start | bytes 25165824 | tf_op jit(solution)/shard_map/all_gather | solution.py:41
  1293.7 297.4 %all-gather.23.cloned.1.call-start = ((), (), s32[]{:S(2)}) async-start(), calls=%async_computation.21 | async-start | bytes 25165824 | tf_op jit(solution)/shard_map/all_gather | solution.py:41
  1397.4 224.1 %all-gather.17.cloned.1.call-start = ((), (), s32[]{:S(2)}) async-start(), calls=%async_computation.16 | async-start | bytes 25165824 | tf_op jit(solution)/shard_map/all_gather | solution.py:41
  1621.5 26.5 %slice-start.4 = ((s8[16777216]{0:T(1024)(128)(4,1)}), s8[4194304]{0:T(1024)(128)(4,1)S(1)}, s32[]{:S(2)}) async-start(s8[16777216]{0:T(1024)(128)(4,1)} %bitcast.25), calls=%async_computation.36 | async-start | bytes 8388608
  1621.5 26.5 %slice-start.5 = ((s8[16777216]{0:T(1024)(128)(4,1)}), s8[4194304]{0:T(1024)(128)(4,1)S(1)}, s32[]{:S(2)}) async-start(s8[16777216]{0:T(1024)(128)(4,1)} %bitcast.25), calls=%async_computation.37 | async-start | bytes 8388608
  1634.5 13.5 slice-start.6
  1634.5 13.5 slice-start.7
  1634.5 22.1 %slice-start = ((s8[16777216]{0:T(1024)(128)(4,1)}), s8[4194304]{0:T(1024)(128)(4,1)S(1)}, s32[]{:S(2)}) async-start(s8[16777216]{0:T(1024)(128)(4,1)} %bitcast.23), calls=%async_computation.32 | async-start | bytes 8388608
  1634.5 22.1 %slice-start.1 = ((s8[16777216]{0:T(1024)(128)(4,1)}), s8[4194304]{0:T(1024)(128)(4,1)S(1)}, s32[]{:S(2)}) async-start(s8[16777216]{0:T(1024)(128)(4,1)} %bitcast.23), calls=%async_computation.33 | async-start | bytes 8388608
  1648.0 10.3 slice-start.2
  1648.0 11.5 slice-start.3
Sparse Core Ops, SparseCore 0:
  252.0 98.8 reduce-scatter.20
  353.8 96.4 reduce-scatter.16
  453.1 96.4 reduce-scatter.12
  552.3 96.4 reduce-scatter.8
  650.9 51.4 reduce-scatter.22
  704.5 51.5 reduce-scatter.18
  758.3 51.4 reduce-scatter.14
  812.1 51.4 reduce-scatter.10
  865.1 54.1 all-gather.30
  920.7 54.1 all-gather.24
  976.4 54.1 all-gather.18
  1032.0 54.1 all-gather.12
  1087.7 102.2 all-gather.32
  1191.4 102.2 all-gather.26
  1295.0 102.2 all-gather.20
  1398.7 102.2 all-gather.14
  1502.4 27.8 all-gather.34
  1531.6 28.9 all-gather.28
  1562.1 28.9 all-gather.22
  1592.5 28.9 all-gather.16
where the time goes:
time: 1680 us; the launch traced here: 1670 us
  waiting for transfers between devices  1120 us (67%)
  matrix products  394 us (23%)
  blocking collectives  60.4 us (4%)
  local copies, waits for them, and re-layouts  44.1 us (3%)
  other arithmetic  39.3 us (2%)
    all_gather x4, waiting for transfers between devices, reduce_grad(): full_sum = lax.all_gather(full_sum, 'second', axis=0, tiled=True)  415 us
    all_gather x4, waiting for transfers between devices, reduce_grad(): full_sum = lax.all_gather(part_sum, 'third', axis=0, tiled=True)  222 us
    reduce_scatter x4, waiting for transfers between devices, reduce_grad(): lax.psum_scatter(part_sum, 'third', scatter_dimension=0, tiled=True)  215 us
    reduce_scatter x4, waiting for transfers between devices, reduce_grad(): lax.psum_scatter(part_sum, 'second', scatter_dimension=0, tiled=True)  190 us
    dot_general x2, matrix products, block_backward(): lax.dot_general(grad_y, w_out, CONTRACT_COLS, preferred_element_type=jnp....  130 us
    dot_general x2, matrix products, block_backward(): lax.dot_general(hidden, grad_y, CONTRACT_ROWS, preferred_element_type=jnp...  91 us
    dot_general x2, matrix products, block_backward(): lax.dot_general(x_in, grad_pre, CONTRACT_ROWS, preferred_element_type=jnp...  86.2 us
    dot_general x2, matrix products, block_backward(): lax.dot_general(grad_pre, w_in, CONTRACT_COLS, preferred_element_type=jnp...  86 us
  transfers between devices with their start and end apart: 20, of which 17 were waited for; matrix products, arithmetic and copies ran while one was open for 12% of the time, Pallas kernels for 0%

commit v1 on v0

v1 whole, which is shorter than its diff:
```python
import functools
import math
import jax
import jax.numpy as jnp
from jax import lax
from jax.experimental import pallas as pl
from jax.experimental.pallas import tpu as pltpu
from jax.sharding import PartitionSpec as P

AXES = ('third', 'second', 'group')
INV_ROOT_TWO = math.sqrt(0.5)
INV_ROOT_TWO_PI = 1.0 / math.sqrt(2.0 * math.pi)
MESH = pl.DeviceIdType.MESH
F32 = jnp.float32
BF16 = jnp.bfloat16
TOK, D, FF = 4096, 1024, 4096
FB = 256
NF = FF // FB
NC = 2 * NF
TM = 256
TN = 256
PART = (FB // 4, D // 4)
COLS = (D, FB)
R1, R2, SD, RS = 5, 4, 4, 8


def kernel(x1, z1, x2, z2, dy, w1i, w1o, w2i, w2o, out_o, out_i, dx_out,
           gbuf, xbuf, acc, zbuf, wobuf, wibuf, wot, wit, ht, dzt,
           slab_a, slab_b, got_a, got_b, part_a, part_b, swp_a, swp_b, sum_a, sum_b,
           gsem, xsem, zsem, wosem, wisem, s1, r1, s2, r2, lsem, s3, r3, sf, rf):
    t, s, g = [lax.axis_index(k) for k in AXES]
    near_axis = (s, t)

    def peer(color, flip_one, flip_two, flip_core):
        ft, fs = (flip_two, flip_one) if color == 0 else (flip_one, flip_two)
        return (1 - t if ft else t, 1 - s if fs else s, 1 - g if flip_core else g)

    slab, got, part = (slab_a, slab_b), (got_a, got_b), (part_a, part_b)
    swp, sums = (swp_a, swp_b), (sum_a, sum_b)

    def quarter_of(color, flip_one, flip_core):
        a = near_axis[color]
        return 2 * (1 - a if flip_one else a) + (1 - g if flip_core else g)

    def slab_rows(color, q):
        return pl.ds(pl.multiple_of(q * PART[color], PART[color]), PART[color])

    def first(c, color, k):
        one, core = ((1, 0), (1, 1), (0, 1))[k]
        return pltpu.make_async_remote_copy(
            src_ref=slab[color].at[c % 2, slab_rows(color, quarter_of(color, one, core))],
            dst_ref=got[color].at[c % R1, k],
            send_sem=s1.at[color, c % 2, k], recv_sem=r1.at[color, c % R1, k],
            device_id=peer(color, one, 0, core), device_id_type=MESH)

    def second(c, color):
        return pltpu.make_async_remote_copy(
            src_ref=part[color].at[c % 2], dst_ref=swp[color].at[c % R2],
            send_sem=s2.at[color, c % 2], recv_sem=r2.at[color, c % R2],
            device_id=peer(color, 0, 1, 0), device_id_type=MESH)

    def region(c, color, q):
        b, f = c // NF, c % NF
        if color == 0:
            row = pl.multiple_of(b * FF + f * FB + q * PART[0], PART[0])
            return out_o.at[pl.ds(row, PART[0])]
        row = pl.multiple_of(b * D + q * PART[1], PART[1])
        return out_i.at[pl.ds(row, PART[1]), pl.ds(pl.multiple_of(f * FB, FB), FB)]

    def local(c, color):
        return pltpu.make_async_copy(sums[color].at[c % SD], region(c, color, quarter_of(color, 0, 0)),
                                     lsem.at[color, c % SD])

    def third(c, color, k):
        return pltpu.make_async_remote_copy(
            src_ref=sums[color].at[c % SD], dst_ref=region(c, color, quarter_of(color, 0, 0)),
            send_sem=s3.at[color, c % SD, k], recv_sem=r3.at[color, c % RS, k],
            device_id=peer(color, 1 - k, 0, k), device_id_type=MESH)

    def forward(c, color):
        there = region(c, color, quarter_of(color, 1, 0))
        return pltpu.make_async_remote_copy(
            src_ref=there, dst_ref=there, send_sem=sf.at[color, c % RS], recv_sem=rf.at[color, c % RS],
            device_id=peer(color, 0, 0, 1), device_id_type=MESH)

    def loads(c, zr, wor, wir):
        f = c % NF
        cols = pl.ds(pl.multiple_of(f * FB, FB), FB)
        k = c % 2
        return (pltpu.make_async_copy(zr.at[:, cols], zbuf.at[k], zsem.at[k]),
                pltpu.make_async_copy(wor.at[cols], wobuf.at[k], wosem.at[k]),
                pltpu.make_async_copy(wir.at[:, cols], wibuf.at[k], wisem.at[k]))

    def start_loads(c):
        @pl.when(c < NF)
        def _():
            for copy in loads(c, z2, w2o, w2i):
                copy.start()

        @pl.when(jnp.logical_and(c >= NF, c < NC))
        def _():
            for copy in loads(c, z1, w1o, w1i):
                copy.start()

    start_loads(0)
    pltpu.make_async_copy(dy, gbuf, gsem).start()
    pltpu.make_async_copy(x2, xbuf, xsem).start()

    barrier = pltpu.get_barrier_semaphore()
    peers = ((0, 1, 0, 0), (0, 1, 0, 1), (1, 1, 0, 0), (1, 1, 0, 1), (0, 0, 0, 1))
    for who in peers:
        pl.semaphore_signal(barrier, inc=1, device_id=peer(*who), device_id_type=MESH)
    pl.semaphore_wait(barrier, len(peers))

    pltpu.make_async_copy(dy, gbuf, gsem).wait()

    def compute(c):
        f = c % NF
        k = c % 2

        @pl.when(c == NF)
        def _():
            pltpu.make_async_copy(x1, xbuf, xsem).start()

        start_loads(c + 1)

        @pl.when(f == 0)
        def _():
            @pl.loop(0, TOK // TM)
            def _(r):
                rows = pl.ds(pl.multiple_of(r * TM, TM), TM)
                acc[rows, :] = gbuf[rows, :].astype(F32)

        for copy in loads(c, z2, w2o, w2i):
            copy.wait()
        wot[...] = wobuf[k].T
        wit[...] = wibuf[k].T

        @pl.loop(0, TOK // TM)
        def _(r):
            rows = pl.ds(pl.multiple_of(r * TM, TM), TM)
            z_val = zbuf[k, rows, :].astype(F32)
            cdf_val = 0.5 * (1.0 + lax.erf(z_val * INV_ROOT_TWO))
            ht[:, rows] = (z_val * cdf_val).astype(BF16).T
            slope = cdf_val + z_val * jnp.exp(-0.5 * z_val * z_val) * INV_ROOT_TWO_PI
            grad_hidden = jnp.dot(gbuf[rows, :], wot[...], preferred_element_type=F32)
            grad_pre = (grad_hidden * slope).astype(BF16)
            dzt[:, rows] = grad_pre.T
            acc[rows, :] += jnp.dot(grad_pre, wit[...], preferred_element_type=F32)

        @pl.when(f == 0)
        def _():
            pltpu.make_async_copy(x2, xbuf, xsem).wait()

        @pl.loop(0, D // TN)
        def _(n):
            cols = pl.ds(pl.multiple_of(n * TN, TN), TN)
            slab_a[k, :, cols] = jnp.dot(ht[...], gbuf[:, cols], preferred_element_type=F32).astype(BF16)
            slab_b[k, cols, :] = jnp.dot(dzt[...], xbuf[:, cols], preferred_element_type=F32).T.astype(BF16)

        @pl.when(f == NF - 1)
        def _():
            @pl.loop(0, TOK // TM)
            def _(r):
                rows = pl.ds(pl.multiple_of(r * TM, TM), TM)
                gbuf[rows, :] = acc[rows, :].astype(BF16)

    @pl.loop(0, NC + 6)
    def _(i):
        @pl.when(i < NC)
        def _():
            compute(i)
            for k in range(3):
                for color in range(2):
                    first(i, color, k).start()

        @pl.when(i == NC - 1)
        def _():
            pltpu.make_async_copy(gbuf, dx_out, gsem).start()

        @pl.when(jnp.logical_and(i >= 1, i < NC + 1))
        def _():
            c = i - 1
            for color in range(2):
                for k in range(3):
                    copy = first(c, color, k)
                    copy.wait_recv()
                    copy.wait_send()
                own = slab[color][c % 2, slab_rows(color, quarter_of(color, 0, 0)), :].astype(F32)
                near, far, pair = [got[color][c % R1, k].astype(F32) for k in range(3)]
                part[color][c % 2] = (own + pair) + (near + far)
                second(c, color).start()

        @pl.when(jnp.logical_and(i >= 2, i < NC + 2))
        def _():
            c = i - 2
            for color in range(2):
                copy = second(c, color)
                copy.wait_recv()
                copy.wait_send()
                sums[color][c % SD] = part[color][c % 2] + swp[color][c % R2]
            for color in range(2):
                for k in range(2):
                    third(c, color, k).start()
                local(c, color).start()

        @pl.when(jnp.logical_and(i >= 4, i < NC + 4))
        def _():
            c = i - 4
            for color in range(2):
                third(c, color, 0).wait_recv()
                forward(c, color).start()

        @pl.when(jnp.logical_and(i >= 5, i < NC + 5))
        def _():
            c = i - 5
            for color in range(2):
                third(c, color, 1).wait_recv()
                third(c, color, 0).wait_send()
                third(c, color, 1).wait_send()
                local(c, color).wait()
                forward(c, color).wait_send()
                forward(c, color).wait_recv()

    pltpu.make_async_copy(gbuf, dx_out, gsem).wait()


def solution(mesh):
    def device_step(x_one, z_one, x_two, z_two, grad_out, w1_in, w1_out, w2_in, w2_out):
        dma = pltpu.SemaphoreType.DMA
        out_o, out_i, dx_one = pl.pallas_call(
            kernel,
            out_shape=(jax.ShapeDtypeStruct((2 * FF, D), F32), jax.ShapeDtypeStruct((2 * D, FF), F32),
                       jax.ShapeDtypeStruct((TOK, D), BF16)),
            in_specs=[pl.BlockSpec(memory_space=pl.ANY)] * 9,
            out_specs=[pl.BlockSpec(memory_space=pl.ANY)] * 3,
            scratch_shapes=[
                pltpu.VMEM((TOK, D), BF16), pltpu.VMEM((TOK, D), BF16), pltpu.VMEM((TOK, D), F32),
                pltpu.VMEM((2, TOK, FB), BF16), pltpu.VMEM((2, FB, D), BF16), pltpu.VMEM((2, D, FB), BF16),
                pltpu.VMEM((D, FB), BF16), pltpu.VMEM((FB, D), BF16),
                pltpu.VMEM((FB, TOK), BF16), pltpu.VMEM((FB, TOK), BF16),
                pltpu.VMEM((2, FB, D), BF16), pltpu.VMEM((2, D, FB), BF16),
                pltpu.VMEM((R1, 3, PART[0], D), BF16), pltpu.VMEM((R1, 3, PART[1], FB), BF16),
                pltpu.VMEM((2, PART[0], D), F32), pltpu.VMEM((2, PART[1], FB), F32),
                pltpu.VMEM((R2, PART[0], D), F32), pltpu.VMEM((R2, PART[1], FB), F32),
                pltpu.VMEM((SD, PART[0], D), F32), pltpu.VMEM((SD, PART[1], FB), F32),
                dma, dma, dma((2,)), dma((2,)), dma((2,)),
                dma((2, 2, 3)), dma((2, R1, 3)), dma((2, 2)), dma((2, R2)),
                dma((2, SD)), dma((2, SD, 2)), dma((2, RS, 2)), dma((2, RS)), dma((2, RS)),
            ],
            compiler_params=pltpu.CompilerParams(collective_id=0, has_side_effects=True,
                                                 vmem_limit_bytes=67043328),
        )(x_one, z_one, x_two, z_two, grad_out, w1_in, w1_out, w2_in, w2_out)
        return out_o[:FF], out_i[:D], out_o[FF:], out_i[D:], dx_one

    row_spec = P(AXES, None)
    repl_spec = P()
    return jax.shard_map(
        device_step,
        mesh=mesh,
        in_specs=(row_spec, row_spec, row_spec, row_spec, row_spec, repl_spec, repl_spec, repl_spec, repl_spec),
        out_specs=(repl_spec, repl_spec, repl_spec, repl_spec, row_spec),
        check_vma=False,
    )
```

time: 1680 us -> 684 us (0.41)
  waiting for transfers between devices: 1120 us -> 0 us
  Pallas kernels: 0 us -> 632 us
  matrix products: 394 us -> 0 us
  blocking collectives: 60.4 us -> 0 us
  other arithmetic: 39.3 us -> 0 us
    all_gather x12 -> x0, waiting for transfers between devices: 714 us -> none  [the longest x4 415 us: reduce_grad(): full_sum = lax.all_gather(full_sum, 'second', axis=0, tiled=True)]
    pallas_call x0 -> x1, Pallas kernels: none -> 632 us  [device_step(): pl.pallas_call(kernel, out_shape=(jax.ShapeDtypeStruct((2 * FF, D), F32),...]
    reduce_scatter x8 -> x0, waiting for transfers between devices: 404 us -> none  [the longest x4 215 us: reduce_grad(): lax.psum_scatter(part_sum, 'third', scatter_dimension=0, tiled=True)]
    dot_general x8 -> x0, matrix products: 394 us -> none  [the longest x2 130 us: block_backward(): lax.dot_general(grad_y, w_out, CONTRACT_COLS, preferred_element_type=jnp....]
    all_to_all x4 -> x0, blocking collectives: 60.4 us -> none  [reduce_grad(): received = lax.all_to_all(pieces, 'group', 0, 0)]
    slice x0 -> x2, local copies, waits for them, and re-layouts: none -> 43.3 us  [device_step(): return (out_o[:FF], out_i[:D], out_o[FF:], out_i[D:], dx_one)]
    reduce_sum x4 -> x0, other arithmetic: 39.3 us -> none  [reduce_grad(): part_sum = jnp.sum(received, axis=0, dtype=jnp.float32)]
    unnamed x20 -> x1, local copies, waits for them, and re-layouts: 44.1 us -> 7.76 us
  transfers between devices with their start and end apart: 20 -> 0, of which waited for: 17 -> 0; matrix products, arithmetic and copies ran while one was open for 12% -> 0% of each run, Pallas kernels for 0% -> 0%
where the time goes in v1:
time: 684 us
  Pallas kernels  632 us (92%)
  local copies, waits for them, and re-layouts  51.1 us (7%)
    pallas_call x1, Pallas kernels, device_step(): pl.pallas_call(kernel, out_shape=(jax.ShapeDtypeStruct((2 * FF, D), F32),...  632 us
    slice x2, local copies, waits for them, and re-layouts, device_step(): return (out_o[:FF], out_i[:D], out_o[FF:], out_i[D:], dx_one)  43.3 us

profile of v1, /device:TPU:0, one launch (start us, length us, event | category | flops | bytes accessed | tf_op | source)
XLA Modules:
  0.0 683.7 jit_solution(6409656116516254149)
XLA Ops:
  0.6 632.0 %shard_map.128 = (f32[8192,1024]{1,0:T(8,128)}, f32[2048,4096]{1,0:T(8,128)}, bf16[4096,1024]{1,0:T(8,128)(2,1)}) custom-call(bf16[4096,1024]{1,0:T(8,128)(2,1)} %x1.1, bf16[4096,4096]{1,0:T(8,128)(2,1)} %z1.1, bf16[4096,1024]{1,0:T(8,128)(2,1)} %x2.1, bf16[4096,4096]{1,0:T(8,128)(2,1)} %z2.1, bf16[4096,1024]{1,0:T(8,128)(2,1)} %dy.1, ...), custom_call_target="tpu_custom_call" | custom-call | tf_op jit(solution)/shard_map/pallas_call | solution.py:231
  632.7 21.9 %fusion.1 = (f32[4096,1024]{1,0:T(8,128)}, f32[4096,1024]{1,0:T(8,128)}) fusion(f32[8192,1024]{1,0:T(8,128)} %get-tuple-element.8), kind=kLoop, calls=%fused_computation.1 | loop fusion | bytes 67108864 | tf_op jit(solution)/shard_map/slice | solution.py:254
  654.6 21.4 %fusion = (f32[1024,4096]{1,0:T(8,128)}, f32[1024,4096]{1,0:T(8,128)}) fusion(f32[2048,4096]{1,0:T(8,128)} %get-tuple-element.9), kind=kLoop, calls=%fused_computation | loop fusion | bytes 67108864 | tf_op jit(solution)/shard_map/slice | solution.py:254
  676.0 7.8 %copy.15 = bf16[4096,1024]{1,0:T(8,128)(2,1)} copy(bf16[4096,1024]{1,0:T(8,128)(2,1)} %get-tuple-element.24) | data formatting | bytes 16777216
